TPU v7x, 32 devices: a whole 2x2x4 slice. The times are simulated.
32 devices in a mesh: pod: 2 (over x), data: 4 (over z), expert: 4 (over y, core).
Axes of the slice: x: 2, y: 2, z: 4, core: 2. Of those that a mesh axis runs over, the one named last changes fastest.
Arguments:
- tokens: bfloat16 [16384, 1024], P(('pod', 'data', 'expert')), parts along dimension 0
- routes: int32 [16384, 8], P(('pod', 'data', 'expert')), parts along dimension 0
- gates: float32 [16384, 8], P(('pod', 'data', 'expert')), parts along dimension 0
- grad_y: bfloat16 [16384, 1024], P(('pod', 'data', 'expert')), parts along dimension 0
- w_in1: bfloat16 [32, 1024, 512], P('expert')
- w_in3: bfloat16 [32, 1024, 512], P('expert')
- w_out: bfloat16 [32, 512, 1024], P('expert')
Outputs:
- output 1: bfloat16 [16384, 1024], P(('pod', 'data', 'expert')), parts along dimension 0
- output 2: bfloat16 [16384, 1024], P(('pod', 'data', 'expert')), parts along dimension 0
- output 3: float32 [64, 1024, 512], P(('pod', 'expert')), parts along dimension 0
- output 4: float32 [64, 1024, 512], P(('pod', 'expert')), parts along dimension 0
- output 5: float32 [64, 512, 1024], P(('pod', 'expert')), parts along dimension 0
There are 2 independent parts. A program takes and returns all parts, laid end to end along the dimension named above; an argument that names none is the same for every part.
All inputs are finite; a program needn't handle non-finite values.
Results may differ from a plain program's by a relative error of at most 0.0106931.
Values are sent between devices in bfloat16 or wider.
A program may use at most 1 GiB of HBM per device.

v0:
```python
import functools

import jax
import jax.numpy as jnp
from jax import lax
from jax.experimental import pallas as pl
from jax.experimental.pallas import tpu as pltpu
from jax.sharding import PartitionSpec as P

MESH = pl.DeviceIdType.MESH
BLOCKS = ("other", "far", "far_o", "z1", "z1_o", "z1y", "z1y_o", "z2", "z2_o", "z2y", "z2y_o", "z3", "z3_o", "z3y", "z3y_o")
N_HOT = 2
RG_ROWS = 16
F32, BF16 = jnp.float32, jnp.bfloat16


def caps(tok_dev, top_k, n_exp):
    cap_hot = 3 * tok_dev // 8
    cap_cold = max(8, ((tok_dev * top_k - N_HOT * cap_hot) // (n_exp - N_HOT) + 7) // 8 * 8)
    return cap_cold, cap_hot


def dot_nn(a, b):
    return lax.dot_general(a, b, (((1,), (0,)), ((), ())), preferred_element_type=F32)


def dot_nt(a, b):
    return lax.dot_general(a, b, (((1,), (1,)), ((), ())), preferred_element_type=F32)


def dot_tn(a, b):
    return lax.dot_general(a, b, (((0,), (0,)), ((), ())), preferred_element_type=F32)


def prefix(m):
    lane = lax.broadcasted_iota(jnp.int32, m.shape, 1)
    step = 1
    while step < m.shape[1]:
        m = m + jnp.where(lane >= step, pltpu.roll(m, step, 1), 0.0)
        step *= 2
    return m


class Engine:
    def __init__(self, cfg, lead, weights, bases, outs, scratch, group):
        self.__dict__.update(cfg)
        self.lead, self.weights, self.bases, self.outs, self.group = lead, weights, bases, outs, group
        (self.rows_x, self.rows_d, self.meta, self.buf, self.hid, self.dab, self.w13, self.w2, self.g13, self.g2,
         self.src_sem, self.w_sem, self.in_sem, self.out_sem) = scratch[:14]
        self.own_scratch = scratch[14:]
        hot = jnp.logical_or(lead * self.n_loc == 0, lead * self.n_loc == self.n_exp // 2)
        self.far = jnp.where(hot, float(self.cap), float(2 * self.tok))
        self.cold, self.part = self.n_loc * self.cap, group * self.cap

    def triple(self, both, single, slot):
        f = self.d_ff
        return both.at[slot, :, 0:f], both.at[slot, :, f:2 * f], single.at[slot]

    def load_w(self, e):
        slot = lax.rem(e, 2)
        return [pltpu.make_async_copy(w.at[e], b, self.w_sem.at[slot, k])
                for k, (w, b) in enumerate(zip(self.weights, self.triple(self.w13, self.w2, slot)))]

    def load_g(self, e):
        slot = lax.rem(e, 4)
        return [pltpu.make_async_copy(w.at[e], b, self.in_sem.at[slot, k])
                for k, (w, b) in enumerate(zip(self.bases, self.triple(self.g13, self.g2, slot)))]

    def save_g(self, e):
        slot = lax.rem(e, 4)
        return [pltpu.make_async_copy(b, w.at[e], self.out_sem.at[slot, k])
                for k, (w, b) in enumerate(zip(self.outs, self.triple(self.g13, self.g2, slot)))]

    def fetches(self, s, ref):
        if not isinstance(ref, tuple):
            return [pltpu.make_async_copy(ref, self.buf.at[s], self.src_sem.at[s, 0])]
        dst = self.buf.at[s]
        return [pltpu.make_async_copy(r, dst.at[pl.ds(at, r.shape[0])], self.src_sem.at[s, k])
                for k, (r, at) in enumerate(zip(ref, (0, self.tok, 2 * self.tok)))]

    def match_rows(self, src, i, base, size):
        iota = lax.broadcasted_iota(jnp.int32, (size, self.tok), 0).astype(F32) + base
        return iota == self.meta[src, pl.ds(i, 1), :]

    def ranks(self, s):
        tok = self.tok
        rg = self.buf[s, 2 * tok:2 * tok + RG_ROWS, :].astype(F32)
        routes = rg[0:8, :tok]
        gates = (rg[8:16, :tok] + rg[0:8, tok:]) + rg[8:16, tok:]
        member, weight = [], []
        for i in range(self.n_loc):
            match = routes == (self.lead * self.n_loc + i).astype(F32)
            member.append(jnp.sum(jnp.where(match, 1.0, 0.0), axis=0, keepdims=True))
            weight.append(jnp.sum(jnp.where(match, gates, 0.0), axis=0, keepdims=True))
        member = jnp.concatenate(member, axis=0)
        self.meta[s, 0:8, :] = jnp.where(member > 0.0, prefix(member) - 1.0, -1.0)
        self.meta[s, 8:16, :] = jnp.concatenate(weight, axis=0)

    def gather(self, s, which):
        tok, meta, buf = self.tok, self.meta, self.buf
        pick, gate = [], []
        for i, base, at, size in which:
            match = self.match_rows(s, i, base, size)
            pick.append(jnp.where(match, 1.0, 0.0).astype(BF16))
            gate.append(jnp.sum(jnp.where(match, meta[s, pl.ds(8 + i, 1), :], 0.0), axis=1, keepdims=True))
        pick, gate = jnp.concatenate(pick, axis=0), jnp.concatenate(gate, axis=0)
        at, size = which[0][2], pick.shape[0]
        self.rows_x[s, at:at + size, :] = dot_nn(pick, buf[s, 0:tok, :]).astype(BF16)
        self.rows_d[s, at:at + size, :] = (dot_nn(pick, buf[s, tok:2 * tok, :]) * gate).astype(BF16)

    def block(self, n_src, n_own, at, size, keep, w, g, g_in):
        d_model, d_ff, hid, dab = self.d_model, self.d_ff, self.hid, self.dab
        w13, w2 = self.w13.at[w], self.w2.at[w]
        rows = n_src * size

        def load(ref):
            return ref[0:n_src, pl.ds(at, size), :].reshape(rows, d_model)

        ab = dot_nn(load(self.rows_x), w13[...]).astype(BF16).astype(F32)
        dh = dot_nt(load(self.rows_d), w2[...])
        a, b = ab[:, :d_ff], ab[:, d_ff:]
        sig = 0.5 * jnp.tanh(0.5 * a) + 0.5
        act = a * sig
        hid[0:rows, :] = (act * b).astype(BF16)
        dab[0:rows, 0:d_ff] = (dh * b * sig * (1.0 + a * (1.0 - sig))).astype(BF16)
        dab[0:rows, d_ff:] = (dh * act).astype(BF16)
        if size < self.cap:
            def columns(k, carry):
                cols = pl.ds(pl.multiple_of(k * d_ff, d_ff), d_ff)
                self.g13[g, :, cols] = self.g13[g, :, cols] + dot_tn(load(self.rows_x), dab[0:rows, cols])
                self.g2[g, :, cols] = self.g2[g, :, cols] + dot_tn(hid[0:rows, :], self.rows_d[0:n_src, pl.ds(at, size), cols].reshape(rows, d_ff))
                return carry

            lax.fori_loop(0, 2, columns, 0)
        else:
            for out, lhs, rhs in ((self.g13, load(self.rows_x), dab[0:rows, :]), (self.g2, hid[0:rows, :], load(self.rows_d))):
                if g_in:
                    out[g] = out[g] + dot_tn(lhs, rhs)
                else:
                    out[g] = dot_tn(lhs, rhs)
        if n_own:
            kept_o, kept_x = self.own_scratch[:2]
            m = n_own * size
            o = dot_nn(hid[0:m, :], w2[...]).astype(BF16)
            dx = dot_nt(dab[0:m, :], w13[...]).astype(BF16)
            kept_o[:, pl.ds(keep, size), :] = o.reshape(n_own, size, d_model)
            kept_x[:, pl.ds(keep, size), :] = dx.reshape(n_own, size, d_model)

    def stage(self, srcs, n_own, first, last, before, held, events, ship, each=None, prelude=lambda: None):
        n_src, n_loc, cap, group = len(srcs), self.n_loc, self.cap, self.group
        width = 1 if n_src == 2 else 2
        turns = n_src // width
        fetch = [self.fetches(s, r) for s, r in enumerate(srcs)]

        def ask(t):
            for s in range(t, n_src, turns):
                before[s]()
                start(fetch[s])

        eager = all(b is nothing for b in before)
        for t in range(turns if eager else 1):
            ask(t)
        prelude()

        def wave(p, carry):
            def turn(t, carry):
                some = [t + j * turns for j in range(width)]

                @pl.when(p == 0)
                def _():
                    for k in range(turns):
                        @pl.when(t == k)
                        def _(k=k):
                            for s in range(k, n_src, turns):
                                wait(fetch[s])
                    for s in some:
                        self.ranks(s)
                        self.gather(s, [(0, self.far, self.part, self.extra)])
                    for k in range(0 if eager else turns - 1):
                        @pl.when(t == k)
                        def _(k=k):
                            ask(k + 1)

                for s in some:
                    self.gather(s, [(group * p + i, 0.0, i * cap, cap) for i in range(group)])
                return carry

            lax.fori_loop(0, turns, turn, 0)

            def one(i, carry):
                e = group * p + i
                wait(self.load_w(e))
                if last:
                    @pl.when(e + 1 < n_loc)
                    def _():
                        start(self.load_w(e + 1))
                else:
                    start(self.load_w(lax.rem(e + 1, n_loc)))

                @pl.when(e >= 2)
                def _():
                    wait(self.save_g(e - 2))

                for k, copies in enumerate(held):
                    @pl.when(e == k)
                    def _(copies=copies):
                        wait(copies)

                if first:
                    @pl.when(e + 2 >= n_loc)
                    def _():
                        start(self.load_g(e + 2 - n_loc))
                elif last:
                    @pl.when(e + 2 < n_loc)
                    def _():
                        start(self.load_g(e + 2))
                else:
                    start(self.load_g(lax.rem(e + 2, n_loc)))
                if not first:
                    wait(self.load_g(e))
                self.block(n_src, n_own, pl.multiple_of(i * cap, cap), cap, pl.multiple_of(e * cap, cap),
                           lax.rem(e, 2), lax.rem(e, 4), not first)

                @pl.when(e == 0)
                def more():
                    self.block(n_src, n_own, self.part, self.extra, self.cold, 0, 0, True)

                start(self.save_g(e))
                for k, event in events:
                    @pl.when(e == k)
                    def _(event=event):
                        event()
                if each is not None:
                    each(e)
                return carry

            lax.fori_loop(0, group, one, 0)
            return carry

        lax.fori_loop(0, n_loc // group, wave, 0)
        if n_own:
            self.combine(n_own, ship)
        elif last:
            wait(self.save_g(n_loc - 2))
            wait(self.save_g(n_loc - 1))

    def combine(self, n_own, ship):
        kept_o, kept_x = self.own_scratch[:2]
        cold, extra, cap, tok, n_loc = self.cold, self.extra, self.cap, self.tok, self.n_loc
        part, n_blk = self.part, n_loc // self.group
        pieces = [(i, 0.0, i // self.group, i % self.group * cap, cap) for i in range(n_loc)] + [(0, self.far, None, part, extra)]
        places = [(ref, pl.ds(lane * tok, tok)) for ref in (self.rows_x, self.rows_d) for lane in (0, 1)]

        def one(src, carry):
            for s in range(n_own):
                @pl.when(src == s)
                def _(s=s):
                    wait(self.save_g(n_loc - 2 + s))

            for i, base, blk, at, size in pieces:
                match = self.match_rows(src, i, base, size)
                gate = self.meta[src, 8 + i:9 + i, :]
                hi = gate.astype(BF16).astype(F32)
                mid = (gate - hi).astype(BF16).astype(F32)
                low = gate - hi - mid
                for k, v in enumerate((hi, mid, low, 1.0)):
                    ref, lanes = places[0 if blk is None else k]
                    ref[k if blk is None else blk, at:at + size, lanes] = jnp.where(match, v, 0.0).astype(BF16)

            def chosen(k):
                ref, lanes = places[k]
                return ref[0:n_blk, 0:part, lanes].reshape(cold, tok)

            spare, lanes = places[0]
            wide = self.d_model // 2

            def columns(h, carry):
                cols = pl.ds(pl.multiple_of(h * wide, wide), wide)
                o, rest = kept_o[src, 0:cold, cols], kept_o[src, cold:cold + extra, cols]
                y = dot_tn(chosen(0), o) + dot_tn(chosen(1), o) + dot_tn(chosen(2), o)
                gates = spare[0:3, part:part + extra, lanes].reshape(3 * extra, tok)
                self.g13[2 + src, 0:tok, cols] = y + dot_tn(gates, jnp.concatenate([rest] * 3, axis=0))
                dx = dot_tn(chosen(3), kept_x[src, 0:cold, cols])
                gates = spare[3, part:part + extra, lanes]
                self.g13[2 + src, tok:2 * tok, cols] = dx + dot_tn(gates, kept_x[src, cold:cold + extra, cols])
                return carry

            lax.fori_loop(0, 2, columns, 0)
            for s in range(n_own):
                @pl.when(src == s)
                def _(s=s):
                    ship[s].start()
            return carry

        lax.fori_loop(0, n_own, one, 0)


def start(copies):
    for c in copies:
        c.start()


def wait(copies):
    for c in copies:
        c.wait()


def nothing():
    pass


class Adder:
    def __init__(self, a, b, out, held, load_sem, save_sem, ready):
        self.a, self.b, self.out, self.held, self.load_sem, self.save_sem, self.ready = a, b, out, held, load_sem, save_sem, ready
        self.rows = held.shape[2]

    def loads(self, k):
        slot, at = lax.rem(k, 2), pl.ds(pl.multiple_of(k * self.rows, self.rows), self.rows)
        return [pltpu.make_async_copy(v.at[at], self.held.at[slot, n], self.load_sem.at[slot, n]) for n, v in enumerate((self.a, self.b))]

    def save(self, k):
        slot, at = lax.rem(k, 2), pl.ds(pl.multiple_of(k * self.rows, self.rows), self.rows)
        return pltpu.make_async_copy(self.held.at[slot, 0], self.out.at[at], self.save_sem.at[slot])

    def add(self, k):
        wait(self.loads(k))
        slot = lax.rem(k, 2)
        self.held[slot, 0] = self.held[slot, 0] + self.held[slot, 1]
        self.save(k).start()

    def __call__(self, e):
        @pl.when(e == 0)
        def _():
            self.ready()

        @pl.when(e >= 1)
        def _():
            self.add(e - 1)

        @pl.when(e >= 2)
        def _():
            self.save(e - 2).wait()

        start(self.loads(e))

    def finish(self, last):
        self.add(last)
        self.save(last - 1).wait()
        self.save(last).wait()


def roam_kernel(cfg, lead_ref, tokens, grad_y, rg, w1, w3, w2, g1, g3, g2, land, own_a, own_b, got_a, got_b, mine, chip, *scratch):
    send_sem, recv_sem, part_sem, held, add_in_sem, add_out_sem = scratch[-6:]
    eng = Engine(cfg, lead_ref[0, 0], (w1, w3, w2), (g1, g3, g2), (g1, g3, g2), scratch[:-6], 2)
    q, r = lax.axis_index("data"), lax.axis_index("expert")
    n_data, n_er, tok, n_loc = cfg["n_data"], cfg["n_er"], cfg["tok"], cfg["n_loc"]
    partner = {"expert": r + 1 - 2 * lax.rem(r, 2)}
    across = {"expert": lax.rem(r + n_er // 2, n_er)}
    znext = {"data": lax.rem(q + 1, n_data)}
    zprev = {"data": lax.rem(q + n_data - 1, n_data)}

    def at(name, rows=None):
        ref = land.at[BLOCKS.index(name)]
        return ref if rows is None else ref.at[rows]

    flights = []

    def remote(src, dst, device):
        k = len(flights)
        copy = pltpu.make_async_remote_copy(src_ref=src, dst_ref=dst, send_sem=send_sem.at[k], recv_sem=recv_sem.at[k],
                                            device_id=device, device_id_type=MESH)
        flights.append(copy)
        return copy

    def first(name, device):
        parts = ((tokens, 0, tok), (grad_y, tok, tok), (rg, 2 * tok, RG_ROWS))
        return [remote(v, at(name, pl.ds(lo, n)), device) for v, lo, n in parts]

    def onward(src, dst, device):
        return [remote(at(src), at(dst), device)]

    upper, lower = pl.ds(0, tok), pl.ds(tok, tok + RG_ROWS)
    c_other, c_far, c_z1 = first("other", partner), first("far", across), first("z1", znext)
    c_far_o, c_z1_o = onward("far", "far_o", partner), onward("z1", "z1_o", partner)
    c_z1y, c_z2 = onward("z1", "z1y", across), onward("z1", "z2", znext)
    c_z1y_o, c_z2_o = onward("z1y", "z1y_o", partner), onward("z2", "z2_o", partner)
    c_z2y, c_z3 = onward("z2", "z2y", across), onward("z2", "z3", znext)
    c_z2y_o, c_z3_o = onward("z2y", "z2y_o", partner), onward("z3", "z3_o", partner)
    c_z3y_z = [remote(at("far", upper), at("z3y", upper), zprev)]
    c_z3y_y = [remote(at("z3", lower), at("z3y", lower), across)]
    c_z3y_zo = [remote(at("z3y", upper), at("z3y_o", upper), partner)]
    c_z3y_yo = [remote(at("z3y", lower), at("z3y_o", lower), partner)]
    c_got_a, c_got_b = [remote(eng.g13.at[3], got_a, partner)], [remote(eng.g13.at[3], got_b, partner)]
    keep_a = pltpu.make_async_copy(eng.g13.at[2], own_a, part_sem.at[0])
    keep_b = pltpu.make_async_copy(eng.g13.at[2], own_b, part_sem.at[1])

    barrier = pltpu.get_barrier_semaphore()
    for device in (partner, across, znext, zprev):
        pl.semaphore_signal(barrier, inc=1, device_id=device, device_id_type=MESH)
    pl.semaphore_wait(barrier, 4)

    class Sent:
        def __init__(self, copy):
            self.copy = copy

        def wait(self):
            self.copy.wait_send()

    def arrived(copies, then=()):
        def event():
            for c in copies:
                c.wait_recv()
            start(then)
        return event

    start(c_other + c_far + c_z1)
    eng.stage([(tokens, grad_y, rg), at("other")], 2, True, False, [nothing, arrived(c_other)], (), (), [keep_a, c_got_a[0]],
              prelude=lambda: start(eng.load_w(0)))
    sum_a = Adder(own_a, got_a, mine, held, add_in_sem, add_out_sem, arrived(c_got_a))
    eng.stage([at("far"), at("far_o"), at("z1"), at("z1_o")], 2, False, False,
              [arrived(c_far, c_far_o), arrived(c_far_o), arrived(c_z1, c_z1_o + c_z1y + c_z2), arrived(c_z1_o)],
              ([keep_a], [Sent(c_got_a[0])]),
              ((6, arrived(c_z1y + c_z2, c_z2y + c_z3 + c_z3y_z + c_z1y_o + c_z2_o)),),
              [keep_b, c_got_b[0]], sum_a)
    sum_a.finish(n_loc - 1)
    sum_b = Adder(own_b, got_b, chip, held, add_in_sem, add_out_sem, arrived(c_got_b))
    eng.stage([at("z1y"), at("z1y_o"), at("z2"), at("z2_o")], 0, False, True,
              [nothing, arrived(c_z1y_o), nothing, arrived(c_z2_o)],
              ([keep_b], [Sent(c_got_b[0])]),
              ((3, arrived(c_z2y + c_z3, c_z3y_y + c_z2y_o + c_z3_o)), (6, arrived(c_z3y_z, c_z3y_zo))), (), sum_b)
    arrived(c_z3y_y, c_z3y_yo)()
    sum_b.finish(n_loc - 1)
    arrived(c_z2y_o + c_z3_o + c_z3y_zo + c_z3y_yo)()
    for c in flights:
        if c is not c_got_a[0] and c is not c_got_b[0]:
            c.wait_send()


def rest_kernel(cfg, lead_ref, land, w1, w3, w2, b1, b3, b2, g1, g3, g2, *scratch):
    eng = Engine(cfg, lead_ref[0, 0], (w1, w3, w2), (b1, b3, b2), (g1, g3, g2), scratch, 2)

    def prelude():
        start(eng.load_w(0))
        for e in (0, 1):
            start(eng.load_g(e))

    names = ("z2y", "z2y_o", "z3", "z3_o", "z3y", "z3y_o")
    eng.stage([land.at[BLOCKS.index(n)] for n in names], 0, False, True, [nothing] * 6, (), (), (), prelude=prelude)


def call_kernel(name, kernel, cfg, args, shapes, n_src, n_own, extra_scratch, params):
    tok, d_model, d_ff, n_loc, cap, extra = (cfg[k] for k in ("tok", "d_model", "d_ff", "n_loc", "cap", "extra"))
    rows = n_loc * cap + extra
    scratch = [pltpu.VMEM((n_src, 2 * cap + extra, d_model), BF16)] * 2 + [
        pltpu.VMEM((n_src, 16, tok), F32),
        pltpu.VMEM((n_src, 2 * tok + RG_ROWS, d_model), BF16),
        pltpu.VMEM((n_src * cap, d_ff), BF16),
        pltpu.VMEM((n_src * cap, 2 * d_ff), BF16),
    ]
    for slots, kind in ((2, BF16), (4, F32)):
        scratch += [pltpu.VMEM((slots, d_model, 2 * d_ff), kind), pltpu.VMEM((slots, d_ff, d_model), kind)]
    scratch += [pltpu.SemaphoreType.DMA(n) for n in ((n_src, 3), (2, 3), (4, 3), (4, 3))]
    if n_own:
        scratch += [pltpu.VMEM((n_own, rows, d_model), BF16)] * 2
    unit = 2 * d_model * d_ff * rows
    return pl.pallas_call(
        functools.partial(kernel, cfg),
        in_specs=[pl.BlockSpec(memory_space=pltpu.SMEM)] + [pl.BlockSpec(memory_space=pl.ANY)] * (len(args) - 1),
        out_specs=[pl.BlockSpec(memory_space=pl.ANY)] * len(shapes),
        out_shape=shapes,
        scratch_shapes=scratch + extra_scratch,
        compiler_params=pltpu.CompilerParams(vmem_limit_bytes=67_000_000, **params),
        cost_estimate=pl.CostEstimate(flops=unit * (8 * n_src + 7 * n_own) // 8, bytes_accessed=100 << 20, transcendentals=0),
        name=name,
    )(*args)


def solution(mesh):
    n_data, n_er = mesh.shape["data"], mesh.shape["expert"]
    row_spec = P(("pod", "data", "expert"), None)
    w_spec = P("expert", None, None)
    grad_spec = P(("pod", "expert"), None, None)
    across = [(r, r ^ 2) for r in range(n_er)]

    def body(tokens, routes, gates, grad_y, w_in1, w_in3, w_out):
        n_loc, d_model, d_ff = w_in1.shape
        n_exp, tok = n_loc * n_er, tokens.shape[0]
        cap, cap_hot = caps(tok, routes.shape[1], n_exp)
        cfg = dict(tok=tok, d_model=d_model, d_ff=d_ff, n_loc=n_loc, n_exp=n_exp, cap=cap, extra=cap_hot - cap,
                   n_data=n_data, n_er=n_er)
        lead = lax.axis_index("expert").astype(jnp.int32).reshape(1, 1)
        gate = gates.T
        hi = lax.reduce_precision(gate, 8, 7)
        mid = lax.reduce_precision(gate - hi, 8, 7)
        low = gate - hi - mid
        rg = jnp.concatenate([jnp.concatenate([routes.T.astype(F32), hi], 0), jnp.concatenate([mid, low], 0)], 1).astype(BF16)
        weights = (w_in1, w_in3, w_out)
        grads = [jax.ShapeDtypeStruct(w.shape, F32) for w in weights]
        sums = [jax.ShapeDtypeStruct((2 * tok, d_model), F32)] * 6
        land = jax.ShapeDtypeStruct((len(BLOCKS), 2 * tok + RG_ROWS, d_model), BF16)
        dma, n_fly = pltpu.SemaphoreType.DMA, 27
        *acc, land, _, _, _, _, mine, chip = call_kernel(
            "roam", roam_kernel, cfg, [lead, tokens, grad_y, rg, *weights], [*grads, land, *sums], 4, 2,
            [dma((n_fly,)), dma((n_fly,)), dma((2,)), pltpu.VMEM((2, 2, 2 * tok // n_loc, d_model), F32), dma((2, 2)), dma((2,))],
            dict(collective_id=0, has_side_effects=True))
        back = lax.ppermute(chip, "expert", across)
        acc1, acc3, acc2 = call_kernel("rest", rest_kernel, cfg, [lead, land, *weights, *acc], grads, 6, 0, [], {})
        y_out = (mine[:tok] + back[:tok]).astype(BF16)
        grad_x = (mine[tok:] + back[tok:]).astype(BF16)
        return y_out, grad_x, acc1, acc3, acc2

    return jax.shard_map(body, mesh=mesh,
                         in_specs=(row_spec, row_spec, row_spec, row_spec, w_spec, w_spec, w_spec),
                         out_specs=(row_spec, row_spec, grad_spec, grad_spec, grad_spec),
                         check_vma=False)
```

profile of v0, /device:TPU:0, one launch (start us, length us, event | category | flops | bytes accessed | tf_op | source)
XLA Modules:
  0.0 296.3 jit_solution(13275356149923056169)
XLA Ops:
  0.6 0.7 fusion.3
  1.4 0.7 reduce-precision_convert_fusion.1
  2.1 0.6 maximum_maximum_fusion.rg
  2.7 195.2 %roam.1 = (f32[8,1024,512]{2,1,0:T(8,128)}, f32[8,1024,512]{2,1,0:T(8,128)}, f32[8,512,1024]{2,1,0:T(8,128)}, bf16[15,1040,1024]{2,1,0:T(8,128)(2,1)}, f32[1024,...) custom-call(s32[1,1]{1,0:T(1,128)} %bitcast.lead_ref, ...), custom_call_target="tpu_custom_call" | custom-call | flops 6559891456 | bytes 104857600 | tf_op jit(solution)/shard_map/roam/pallas_call | solution.py:466
  197.9 1.7 collective-permute-start
  199.6 74.5 %rest.1 = (f32[8,1024,512]{2,1,0:T(8,128)}, f32[8,1024,512]{2,1,0:T(8,128)}, f32[8,512,1024]{2,1,0:T(8,128)}) custom-call(s32[1,1]{1,0:T(1,128)} %bitcast.lead_ref, bf16[15,1040,1024]{2,1,0:T(8,128)(2,1)} %get-tuple-element.16.land, bf16[8,1024,512]{2,1,0:T(8,128)(2,1)} %w1.3, bf16[8,1024,512]{2,1,0:T(8,128)(2,1)} %w3.3, bf16[8,512,1024]{2,1,0:T(8,128)(2,1)} %w2.3, ...), custom_call_target="tpu_custom_call" | custom-call | flops 6845104128 | bytes 104857600 | tf_op jit(solution)/shard_map/rest/pallas_call | solution.py:466
  274.1 16.7 %collective-permute-done = f32[1024,1024]{1,0:T(8,128)} collective-permute-done((f32[1024,1024]{1,0:T(8,128)}, f32[1024,1024]{1,0:T(8,128)}, u32[]{:S(2)}, u32[]{:S(2)}) %collective-permute-start) | collective-permute-done | bytes 4194336 | tf_op jit(solution)/shard_map/ppermute | solution.py:506
  290.8 5.5 %fusion = (bf16[512,1024]{1,0:T(8,128)(2,1)}, bf16[512,1024]{1,0:T(8,128)(2,1)}) fusion(f32[1024,1024]{1,0:T(8,128)} %collective-permute-done, f32[1024,1024]{1,0:T(8,128)} %get-tuple-element.14), kind=kLoop, calls=%fused_computation.1 | loop fusion | flops 2097152 | bytes 10485760 | tf_op jit(solution)/shard_map/convert_element_type | solution.py:509
Async XLA Ops:
  197.9 92.9 %collective-permute-start = (f32[1024,1024]{1,0:T(8,128)}, f32[1024,1024]{1,0:T(8,128)}, u32[]{:S(2)}, u32[]{:S(2)}) collective-permute-start(f32[1024,1024]{1,0:T(8,128)} %get-tuple-element.15), channel_id=1, source_target_pairs={{0,2},{1,3},{2,0},{3,1},{4,6},{5,7},{6,4},{7,5},{8,10},{9,11},{10,... | collective-permute-start | bytes 12582920 | tf_op jit(solution)/shard_map/ppermute | solution.py:506
where the time goes:
time: 297 us; the launch traced here: 296 us
  Pallas kernels  270 us (91%)
  waiting for transfers between devices  16.7 us (6%)
  other arithmetic  7.57 us (3%)
    pallas_call x2, Pallas kernels, call_kernel(): pl.pallas_call(functools.partial(kernel, cfg), in_specs=[pl.BlockSpec(mem...  270 us
    ppermute x1, waiting for transfers between devices, body(): back = lax.ppermute(chip, 'expert', across)  16.7 us
  transfers between devices with their start and end apart: 1, of which 1 were waited for; matrix products, arithmetic and copies ran while one was open for 0% of the time, Pallas kernels for 25%

commit v1 on v0

--- a/solution.py
+++ b/solution.py
@@ -313,20 +313,40 @@
     def __init__(self, a, b, out, held, load_sem, save_sem, ready):
         self.a, self.b, self.out, self.held, self.load_sem, self.save_sem, self.ready = a, b, out, held, load_sem, save_sem, ready
         self.rows = held.shape[2]
+        self.n_head = out[0].shape[0] // self.rows if out[0] is not None else 0
 
     def loads(self, k):
         slot, at = lax.rem(k, 2), pl.ds(pl.multiple_of(k * self.rows, self.rows), self.rows)
         return [pltpu.make_async_copy(v.at[at], self.held.at[slot, n], self.load_sem.at[slot, n]) for n, v in enumerate((self.a, self.b))]
 
-    def save(self, k):
-        slot, at = lax.rem(k, 2), pl.ds(pl.multiple_of(k * self.rows, self.rows), self.rows)
-        return pltpu.make_async_copy(self.held.at[slot, 0], self.out.at[at], self.save_sem.at[slot])
+    def save(self, k, head=False):
+        slot = lax.rem(k, 2)
+        ref, k = (self.out[0], k) if head else (self.out[1], k - self.n_head)
+        at = pl.ds(pl.multiple_of(k * self.rows, self.rows), self.rows)
+        return pltpu.make_async_copy(self.held.at[slot, 0], ref.at[at], self.save_sem.at[slot])
 
     def add(self, k):
         wait(self.loads(k))
         slot = lax.rem(k, 2)
         self.held[slot, 0] = self.held[slot, 0] + self.held[slot, 1]
-        self.save(k).start()
+        if self.n_head:
+            @pl.when(k < self.n_head)
+            def _():
+                self.save(k, True).start()
+
+        @pl.when(k >= self.n_head)
+        def _():
+            self.save(k).start()
+
+    def saved(self, k):
+        if self.n_head:
+            @pl.when(k < self.n_head)
+            def _():
+                self.save(k, True).wait()
+
+        @pl.when(k >= self.n_head)
+        def _():
+            self.save(k).wait()
 
     def __call__(self, e):
         @pl.when(e == 0)
@@ -339,17 +359,17 @@
 
         @pl.when(e >= 2)
         def _():
-            self.save(e - 2).wait()
+            self.saved(e - 2)
 
         start(self.loads(e))
 
     def finish(self, last):
         self.add(last)
-        self.save(last - 1).wait()
-        self.save(last).wait()
-
-
-def roam_kernel(cfg, lead_ref, tokens, grad_y, rg, w1, w3, w2, g1, g3, g2, land, own_a, own_b, got_a, got_b, mine, chip, *scratch):
+        self.saved(last - 1)
+        self.saved(last)
+
+
+def roam_kernel(cfg, lead_ref, tokens, grad_y, rg, w1, w3, w2, g1, g3, g2, land, own_a, own_b, got_a, got_b, mine, chip_a, chip_b, back_a, *scratch):
     send_sem, recv_sem, part_sem, held, add_in_sem, add_out_sem = scratch[-6:]
     eng = Engine(cfg, lead_ref[0, 0], (w1, w3, w2), (g1, g3, g2), (g1, g3, g2), scratch[:-6], 2)
     q, r = lax.axis_index("data"), lax.axis_index("expert")
@@ -379,7 +399,9 @@
     def onward(src, dst, device):
         return [remote(at(src), at(dst), device)]
 
-    upper, lower = pl.ds(0, tok), pl.ds(tok, tok + RG_ROWS)
+    cut = (2 * tok + RG_ROWS) // 64 * 48
+    upper, lower = pl.ds(0, cut), pl.ds(cut, 2 * tok + RG_ROWS - cut)
+    c_back = [remote(chip_a, back_a, across)]
     c_other, c_far, c_z1 = first("other", partner), first("far", across), first("z1", znext)
     c_far_o, c_z1_o = onward("far", "far_o", partner), onward("z1", "z1_o", partner)
     c_z1y, c_z2 = onward("z1", "z1y", across), onward("z1", "z2", znext)
@@ -416,21 +438,21 @@
     start(c_other + c_far + c_z1)
     eng.stage([(tokens, grad_y, rg), at("other")], 2, True, False, [nothing, arrived(c_other)], (), (), [keep_a, c_got_a[0]],
               prelude=lambda: start(eng.load_w(0)))
-    sum_a = Adder(own_a, got_a, mine, held, add_in_sem, add_out_sem, arrived(c_got_a))
+    sum_a = Adder(own_a, got_a, (None, mine), held, add_in_sem, add_out_sem, arrived(c_got_a))
     eng.stage([at("far"), at("far_o"), at("z1"), at("z1_o")], 2, False, False,
               [arrived(c_far, c_far_o), arrived(c_far_o), arrived(c_z1, c_z1_o + c_z1y + c_z2), arrived(c_z1_o)],
               ([keep_a], [Sent(c_got_a[0])]),
-              ((6, arrived(c_z1y + c_z2, c_z2y + c_z3 + c_z3y_z + c_z1y_o + c_z2_o)),),
+              ((6, arrived(c_z1y + c_z2, c_z2y + c_z3 + c_z1y_o + c_z2_o)),),
               [keep_b, c_got_b[0]], sum_a)
     sum_a.finish(n_loc - 1)
-    sum_b = Adder(own_b, got_b, chip, held, add_in_sem, add_out_sem, arrived(c_got_b))
+    sum_b = Adder(own_b, got_b, (chip_a, chip_b), held, add_in_sem, add_out_sem, arrived(c_got_b))
     eng.stage([at("z1y"), at("z1y_o"), at("z2"), at("z2_o")], 0, False, True,
               [nothing, arrived(c_z1y_o), nothing, arrived(c_z2_o)],
               ([keep_b], [Sent(c_got_b[0])]),
-              ((3, arrived(c_z2y + c_z3, c_z3y_y + c_z2y_o + c_z3_o)), (6, arrived(c_z3y_z, c_z3y_zo))), (), sum_b)
-    arrived(c_z3y_y, c_z3y_yo)()
+              ((3, arrived(c_z2y + c_z3, c_z3y_y + c_z3y_z + c_z2y_o + c_z3_o)), (4, lambda: start(c_back)), (6, arrived(c_z3y_y, c_z3y_yo))), (), sum_b)
     sum_b.finish(n_loc - 1)
-    arrived(c_z2y_o + c_z3_o + c_z3y_zo + c_z3y_yo)()
+    arrived(c_z3y_z, c_z3y_zo)()
+    arrived(c_z2y_o + c_z3_o + c_z3y_zo + c_z3y_yo + c_back)()
     for c in flights:
         if c is not c_got_a[0] and c is not c_got_b[0]:
             c.wait_send()
@@ -475,6 +497,38 @@
     )(*args)
 
 
+def last_sum(mine, back_a, back_b, tok, d_model):
+    rows = back_a.shape[0] // 2
+    n_half = tok // rows
+
+    def kernel(m_ref, a_ref, b_ref, y_ref, x_ref):
+        j = pl.program_id(0)
+
+        @pl.when(j < 2)
+        def _():
+            y_ref[...] = (m_ref[...] + a_ref[...]).astype(BF16)
+
+        @pl.when(jnp.logical_and(j >= 2, j < n_half))
+        def _():
+            y_ref[...] = (m_ref[...] + b_ref[...]).astype(BF16)
+
+        @pl.when(j >= n_half)
+        def _():
+            x_ref[...] = (m_ref[...] + b_ref[...]).astype(BF16)
+
+    def spec(index):
+        return pl.BlockSpec((rows, d_model), lambda j: (index(j), 0))
+
+    return pl.pallas_call(
+        kernel,
+        grid=(2 * n_half,),
+        in_specs=[spec(lambda j: j), spec(lambda j: jnp.minimum(j, 1)), spec(lambda j: jnp.maximum(j - 2, 0))],
+        out_specs=[spec(lambda j: jnp.minimum(j, n_half - 1)), spec(lambda j: jnp.maximum(j - n_half, 0))],
+        out_shape=[jax.ShapeDtypeStruct((tok, d_model), BF16)] * 2,
+        name="last",
+    )(mine, back_a, back_b)
+
+
 def solution(mesh):
     n_data, n_er = mesh.shape["data"], mesh.shape["expert"]
     row_spec = P(("pod", "data", "expert"), None)
@@ -498,15 +552,15 @@
         grads = [jax.ShapeDtypeStruct(w.shape, F32) for w in weights]
         sums = [jax.ShapeDtypeStruct((2 * tok, d_model), F32)] * 6
         land = jax.ShapeDtypeStruct((len(BLOCKS), 2 * tok + RG_ROWS, d_model), BF16)
-        dma, n_fly = pltpu.SemaphoreType.DMA, 27
-        *acc, land, _, _, _, _, mine, chip = call_kernel(
+        dma, n_fly, quarter = pltpu.SemaphoreType.DMA, 28, 2 * (2 * tok // n_loc)
+        sums[5:] = [jax.ShapeDtypeStruct((n, d_model), F32) for n in (quarter, 2 * tok - quarter, quarter)]
+        *acc, land, _, _, _, _, mine, _, chip_b, back_a = call_kernel(
             "roam", roam_kernel, cfg, [lead, tokens, grad_y, rg, *weights], [*grads, land, *sums], 4, 2,
             [dma((n_fly,)), dma((n_fly,)), dma((2,)), pltpu.VMEM((2, 2, 2 * tok // n_loc, d_model), F32), dma((2, 2)), dma((2,))],
             dict(collective_id=0, has_side_effects=True))
-        back = lax.ppermute(chip, "expert", across)
+        back_b = lax.ppermute(chip_b, "expert", across)
         acc1, acc3, acc2 = call_kernel("rest", rest_kernel, cfg, [lead, land, *weights, *acc], grads, 6, 0, [], {})
-        y_out = (mine[:tok] + back[:tok]).astype(BF16)
-        grad_x = (mine[tok:] + back[tok:]).astype(BF16)
+        y_out, grad_x = last_sum(mine, back_a, back_b, tok, d_model)
         return y_out, grad_x, acc1, acc3, acc2
 
     return jax.shard_map(body, mesh=mesh,

time: 297 us -> 290 us (0.976)
  waiting for transfers between devices: 16.7 us -> 0.01 us
  Pallas kernels: 270 us -> 285 us
  other arithmetic: 7.57 us -> 2.06 us
    ppermute x1, waiting for transfers between devices: 16.7 us -> 0.01 us  [body(): back_b = lax.ppermute(chip_b, 'expert', across)]
    pallas_call x2, Pallas kernels: 270 us -> 278 us  [call_kernel(): pl.pallas_call(functools.partial(kernel, cfg), in_specs=[pl.BlockSpec(mem...]
    pallas_call x0 -> x1, Pallas kernels: none -> 7.03 us  [last_sum(): pl.pallas_call(kernel, grid=(2 * n_half,), in_specs=[spec(lambda j: j), s...]
    convert_element_type x1 -> x0, other arithmetic: 5.51 us -> none  [body(): grad_x = (mine[tok:] + back[tok:]).astype(BF16)]
  transfers between devices with their start and end apart: 1 -> 1, of which waited for: 1 -> 0; matrix products, arithmetic and copies ran while one was open for 0% -> 0% of each run, Pallas kernels for 25% -> 26%
where the time goes in v1:
time: 290 us; the launch traced here: 289 us
  Pallas kernels  285 us (98%)
    pallas_call x2, Pallas kernels, call_kernel(): pl.pallas_call(functools.partial(kernel, cfg), in_specs=[pl.BlockSpec(mem...  278 us
    pallas_call x1, Pallas kernels, last_sum(): pl.pallas_call(kernel, grid=(2 * n_half,), in_specs=[spec(lambda j: j), s...  7.03 us
  transfers between devices with their start and end apart: 1, of which 0 were waited for; matrix products, arithmetic and copies ran while one was open for 0% of the time, Pallas kernels for 26%

profile of v1, /device:TPU:0, one launch (start us, length us, event | category | flops | bytes accessed | tf_op | source)
XLA Modules:
  0.0 289.2 jit_solution(4518150122746729254)
XLA Ops:
  0.6 0.7 fusion.1
  1.4 0.7 reduce-precision_convert_fusion.1
  2.1 0.6 maximum_maximum_fusion.rg
  2.7 203.4 %roam.1 = (f32[8,1024,512]{2,1,0:T(8,128)}, f32[8,1024,512]{2,1,0:T(8,128)}, f32[8,512,1024]{2,1,0:T(8,128)}, bf16[15,1040,1024]{2,1,0:T(8,128)(2,1)}, f32[1024,...) custom-call(s32[1,1]{1,0:T(1,128)} %bitcast.lead_ref, ...), custom_call_target="tpu_custom_call" | custom-call | flops 6559891456 | bytes 104857600 | tf_op jit(solution)/shard_map/roam/pallas_call | solution.py:488
  206.1 1.6 collective-permute-start
  207.7 74.5 %rest.1 = (f32[8,1024,512]{2,1,0:T(8,128)}, f32[8,1024,512]{2,1,0:T(8,128)}, f32[8,512,1024]{2,1,0:T(8,128)}) custom-call(s32[1,1]{1,0:T(1,128)} %bitcast.lead_ref, bf16[15,1040,1024]{2,1,0:T(8,128)(2,1)} %get-tuple-element.22.land, bf16[8,1024,512]{2,1,0:T(8,128)(2,1)} %w1.3, bf16[8,1024,512]{2,1,0:T(8,128)(2,1)} %w3.3, bf16[8,512,1024]{2,1,0:T(8,128)(2,1)} %w2.3, ...), custom_call_target="tpu_custom_call" | custom-call | flops 6845104128 | bytes 104857600 | tf_op jit(solution)/shard_map/rest/pallas_call | solution.py:488
  282.2 0.0 collective-permute-done.b_ref
  282.2 7.0 %last.1 = (bf16[512,1024]{1,0:T(8,128)(2,1)}, bf16[512,1024]{1,0:T(8,128)(2,1)}) custom-call(f32[1024,1024]{1,0:T(8,128)} %get-tuple-element.17.m_ref, f32[256,1024]{1,0:T(8,128)} %get-tuple-element.18.a_ref, f32[768,1024]{1,0:T(8,128)} %collective-permute-done.b_ref), custom_call_target="tpu_custom_call" | custom-call | tf_op jit(solution)/shard_map/last/pallas_call | solution.py:522
Async XLA Ops:
  206.1 76.1 %collective-permute-start = (f32[768,1024]{1,0:T(8,128)}, f32[768,1024]{1,0:T(8,128)}, u32[]{:S(2)}, u32[]{:S(2)}) collective-permute-start(f32[768,1024]{1,0:T(8,128)} %get-tuple-element.19), channel_id=1, source_target_pairs={{0,2},{1,3},{2,0},{3,1},{4,6},{5,7},{6,4},{7,5},{8,10},{9,11},{10,... | collective-permute-start | bytes 9437192 | tf_op jit(solution)/shard_map/ppermute | solution.py:561

commit v2 on v1

--- a/solution.py
+++ b/solution.py
@@ -108,7 +108,7 @@
         self.rows_x[s, at:at + size, :] = dot_nn(pick, buf[s, 0:tok, :]).astype(BF16)
         self.rows_d[s, at:at + size, :] = (dot_nn(pick, buf[s, tok:2 * tok, :]) * gate).astype(BF16)
 
-    def block(self, n_src, n_own, at, size, keep, w, g, g_in):
+    def block(self, n_src, n_own, at, size, keep, w, g, g_in, middle=lambda: None):
         d_model, d_ff, hid, dab = self.d_model, self.d_ff, self.hid, self.dab
         w13, w2 = self.w13.at[w], self.w2.at[w]
         rows = n_src * size
@@ -124,6 +124,7 @@
         hid[0:rows, :] = (act * b).astype(BF16)
         dab[0:rows, 0:d_ff] = (dh * b * sig * (1.0 + a * (1.0 - sig))).astype(BF16)
         dab[0:rows, d_ff:] = (dh * act).astype(BF16)
+        middle()
         if size < self.cap:
             def columns(k, carry):
                 cols = pl.ds(pl.multiple_of(k * d_ff, d_ff), d_ff)
@@ -176,13 +177,18 @@
                     for s in some:
                         self.ranks(s)
                         self.gather(s, [(0, self.far, self.part, self.extra)])
-                    for k in range(0 if eager else turns - 1):
+                    for k in range(0 if eager or width == 1 else turns - 1):
                         @pl.when(t == k)
                         def _(k=k):
                             ask(k + 1)
 
                 for s in some:
                     self.gather(s, [(group * p + i, 0.0, i * cap, cap) for i in range(group)])
+                if width == 1 and not eager:
+                    for k in range(turns - 1):
+                        @pl.when(jnp.logical_and(p == 0, t == k))
+                        def _(k=k):
+                            ask(k + 1)
                 return carry
 
             lax.fori_loop(0, turns, turn, 0)
@@ -197,29 +203,31 @@
                 else:
                     start(self.load_w(lax.rem(e + 1, n_loc)))
 
-                @pl.when(e >= 2)
-                def _():
-                    wait(self.save_g(e - 2))
-
-                for k, copies in enumerate(held):
-                    @pl.when(e == k)
-                    def _(copies=copies):
-                        wait(copies)
-
-                if first:
-                    @pl.when(e + 2 >= n_loc)
+                def middle():
+                    @pl.when(e >= 2)
                     def _():
-                        start(self.load_g(e + 2 - n_loc))
-                elif last:
-                    @pl.when(e + 2 < n_loc)
-                    def _():
-                        start(self.load_g(e + 2))
-                else:
-                    start(self.load_g(lax.rem(e + 2, n_loc)))
-                if not first:
-                    wait(self.load_g(e))
+                        wait(self.save_g(e - 2))
+
+                    for k, copies in enumerate(held):
+                        @pl.when(e == k)
+                        def _(copies=copies):
+                            wait(copies)
+
+                    if first:
+                        @pl.when(e + 2 >= n_loc)
+                        def _():
+                            start(self.load_g(e + 2 - n_loc))
+                    elif last:
+                        @pl.when(e + 2 < n_loc)
+                        def _():
+                            start(self.load_g(e + 2))
+                    else:
+                        start(self.load_g(lax.rem(e + 2, n_loc)))
+                    if not first:
+                        wait(self.load_g(e))
+
                 self.block(n_src, n_own, pl.multiple_of(i * cap, cap), cap, pl.multiple_of(e * cap, cap),
-                           lax.rem(e, 2), lax.rem(e, 4), not first)
+                           lax.rem(e, 2), lax.rem(e, 4), not first, middle)
 
                 @pl.when(e == 0)
                 def more():
@@ -442,14 +450,14 @@
     eng.stage([at("far"), at("far_o"), at("z1"), at("z1_o")], 2, False, False,
               [arrived(c_far, c_far_o), arrived(c_far_o), arrived(c_z1, c_z1_o + c_z1y + c_z2), arrived(c_z1_o)],
               ([keep_a], [Sent(c_got_a[0])]),
-              ((6, arrived(c_z1y + c_z2, c_z2y + c_z3 + c_z1y_o + c_z2_o)),),
+              ((4, arrived(c_z1y + c_z2, c_z2y + c_z3 + c_z1y_o + c_z2_o)),),
               [keep_b, c_got_b[0]], sum_a)
     sum_a.finish(n_loc - 1)
     sum_b = Adder(own_b, got_b, (chip_a, chip_b), held, add_in_sem, add_out_sem, arrived(c_got_b))
     eng.stage([at("z1y"), at("z1y_o"), at("z2"), at("z2_o")], 0, False, True,
               [nothing, arrived(c_z1y_o), nothing, arrived(c_z2_o)],
               ([keep_b], [Sent(c_got_b[0])]),
-              ((3, arrived(c_z2y + c_z3, c_z3y_y + c_z3y_z + c_z2y_o + c_z3_o)), (4, lambda: start(c_back)), (6, arrived(c_z3y_y, c_z3y_yo))), (), sum_b)
+              ((0, arrived(c_z2y + c_z3, c_z3y_y + c_z3y_z + c_z2y_o + c_z3_o)), (4, lambda: start(c_back)), (6, arrived(c_z3y_y, c_z3y_yo))), (), sum_b)
     sum_b.finish(n_loc - 1)
     arrived(c_z3y_z, c_z3y_zo)()
     arrived(c_z2y_o + c_z3_o + c_z3y_zo + c_z3y_yo + c_back)()
@@ -499,32 +507,35 @@
 
 def last_sum(mine, back_a, back_b, tok, d_model):
     rows = back_a.shape[0] // 2
-    n_half = tok // rows
-
-    def kernel(m_ref, a_ref, b_ref, y_ref, x_ref):
-        j = pl.program_id(0)
-
-        @pl.when(j < 2)
-        def _():
-            y_ref[...] = (m_ref[...] + a_ref[...]).astype(BF16)
-
-        @pl.when(jnp.logical_and(j >= 2, j < n_half))
-        def _():
-            y_ref[...] = (m_ref[...] + b_ref[...]).astype(BF16)
-
-        @pl.when(j >= n_half)
-        def _():
-            x_ref[...] = (m_ref[...] + b_ref[...]).astype(BF16)
-
-    def spec(index):
-        return pl.BlockSpec((rows, d_model), lambda j: (index(j), 0))
-
+    n_all, n_half = 2 * tok // rows, tok // rows
+
+    def kernel(m_ref, a_ref, b_ref, y_ref, x_ref, m, v, out, in_sem, out_sem):
+        def piece(ref, j):
+            return ref.at[pl.ds(j * rows, rows)]
+
+        loads, saves = [], []
+        for j in range(n_all):
+            other = piece(a_ref, j) if j < 2 else piece(b_ref, j - 2)
+            loads.append([pltpu.make_async_copy(piece(m_ref, j), m.at[j], in_sem.at[j, 0]),
+                          pltpu.make_async_copy(other, v.at[j], in_sem.at[j, 1])])
+            place = piece(y_ref, j) if j < n_half else piece(x_ref, j - n_half)
+            saves.append(pltpu.make_async_copy(out.at[j], place, out_sem.at[j]))
+        for copies in loads:
+            start(copies)
+        for j in range(n_all):
+            wait(loads[j])
+            out[j] = (m[j] + v[j]).astype(BF16)
+            saves[j].start()
+        wait(saves)
+
+    dma = pltpu.SemaphoreType.DMA
     return pl.pallas_call(
         kernel,
-        grid=(2 * n_half,),
-        in_specs=[spec(lambda j: j), spec(lambda j: jnp.minimum(j, 1)), spec(lambda j: jnp.maximum(j - 2, 0))],
-        out_specs=[spec(lambda j: jnp.minimum(j, n_half - 1)), spec(lambda j: jnp.maximum(j - n_half, 0))],
+        in_specs=[pl.BlockSpec(memory_space=pl.ANY)] * 3,
+        out_specs=[pl.BlockSpec(memory_space=pl.ANY)] * 2,
         out_shape=[jax.ShapeDtypeStruct((tok, d_model), BF16)] * 2,
+        scratch_shapes=[pltpu.VMEM((n_all, rows, d_model), F32)] * 2 + [pltpu.VMEM((n_all, rows, d_model), BF16), dma((n_all, 2)), dma((n_all,))],
+        compiler_params=pltpu.CompilerParams(vmem_limit_bytes=67_000_000),
         name="last",
     )(mine, back_a, back_b)
 

time: 290 us -> 284 us (0.979)
  Pallas kernels: 285 us -> 279 us
    pallas_call x2, Pallas kernels: 278 us -> 274 us  [call_kernel(): pl.pallas_call(functools.partial(kernel, cfg), in_specs=[pl.BlockSpec(mem...]
where the time goes in v2:
time: 284 us
  Pallas kernels  279 us (98%)
    pallas_call x2, Pallas kernels, call_kernel(): pl.pallas_call(functools.partial(kernel, cfg), in_specs=[pl.BlockSpec(mem...  274 us
  transfers between devices with their start and end apart: 1, of which 0 were waited for; matrix products, arithmetic and copies ran while one was open for 0% of the time, Pallas kernels for 26%

profile of v2, /device:TPU:0, one launch (start us, length us, event | category | flops | bytes accessed | tf_op | source)
XLA Modules:
  0.0 283.7 jit_solution(5411167336675532018)
XLA Ops:
  0.6 0.7 fusion.1
  1.4 0.7 reduce-precision_convert_fusion.1
  2.1 0.6 maximum_maximum_fusion.rg
  2.7 199.8 %roam.1 = (f32[8,1024,512]{2,1,0:T(8,128)}, f32[8,1024,512]{2,1,0:T(8,128)}, f32[8,512,1024]{2,1,0:T(8,128)}, bf16[15,1040,1024]{2,1,0:T(8,128)(2,1)}, f32[1024,...) custom-call(s32[1,1]{1,0:T(1,128)} %bitcast.lead_ref, ...), custom_call_target="tpu_custom_call" | custom-call | flops 6559891456 | bytes 104857600 | tf_op jit(solution)/shard_map/roam/pallas_call | solution.py:496
  202.5 1.6 collective-permute-start
  204.1 74.6 %rest.1 = (f32[8,1024,512]{2,1,0:T(8,128)}, f32[8,1024,512]{2,1,0:T(8,128)}, f32[8,512,1024]{2,1,0:T(8,128)}) custom-call(s32[1,1]{1,0:T(1,128)} %bitcast.lead_ref, bf16[15,1040,1024]{2,1,0:T(8,128)(2,1)} %get-tuple-element.22.land, bf16[8,1024,512]{2,1,0:T(8,128)(2,1)} %w1.3, bf16[8,1024,512]{2,1,0:T(8,128)(2,1)} %w3.3, bf16[8,512,1024]{2,1,0:T(8,128)(2,1)} %w2.3, ...), custom_call_target="tpu_custom_call" | custom-call | flops 6845104128 | bytes 104857600 | tf_op jit(solution)/shard_map/rest/pallas_call | solution.py:496
  278.7 0.0 collective-permute-done.b_ref
  278.7 4.8 %last.1 = (bf16[512,1024]{1,0:T(8,128)(2,1)}, bf16[512,1024]{1,0:T(8,128)(2,1)}) custom-call(f32[1024,1024]{1,0:T(8,128)} %get-tuple-element.17.m_ref, f32[256,1024]{1,0:T(8,128)} %get-tuple-element.18.a_ref, f32[768,1024]{1,0:T(8,128)} %collective-permute-done.b_ref), custom_call_target="tpu_custom_call" | custom-call | tf_op jit(solution)/shard_map/last/pallas_call | solution.py:532
Async XLA Ops:
  202.5 76.2 %collective-permute-start = (f32[768,1024]{1,0:T(8,128)}, f32[768,1024]{1,0:T(8,128)}, u32[]{:S(2)}, u32[]{:S(2)}) collective-permute-start(f32[768,1024]{1,0:T(8,128)} %get-tuple-element.19), channel_id=1, source_target_pairs={{0,2},{1,3},{2,0},{3,1},{4,6},{5,7},{6,4},{7,5},{8,10},{9,11},{10,... | collective-permute-start | bytes 9437192 | tf_op jit(solution)/shard_map/ppermute | solution.py:572

commit v3 on v2

--- a/solution.py
+++ b/solution.py
@@ -162,6 +162,9 @@
         for t in range(turns if eager else 1):
             ask(t)
         prelude()
+        if held:
+            wait(held[0])
+            start(self.load_g(2))
 
         def wave(p, carry):
             def turn(t, carry):
@@ -208,21 +211,25 @@
                     def _():
                         wait(self.save_g(e - 2))
 
-                    for k, copies in enumerate(held):
-                        @pl.when(e == k)
-                        def _(copies=copies):
-                            wait(copies)
+                    if held:
+                        @pl.when(e == 0)
+                        def _():
+                            wait(held[1])
+                            start(self.load_g(3))
 
                     if first:
                         @pl.when(e + 2 >= n_loc)
                         def _():
                             start(self.load_g(e + 2 - n_loc))
-                    elif last:
-                        @pl.when(e + 2 < n_loc)
+                    else:
+                        @pl.when(jnp.logical_and(e >= 2, e + 2 < n_loc))
                         def _():
                             start(self.load_g(e + 2))
-                    else:
-                        start(self.load_g(lax.rem(e + 2, n_loc)))
+
+                        if not last:
+                            @pl.when(e + 2 >= n_loc)
+                            def _():
+                                start(self.load_g(e + 2 - n_loc))
                     if not first:
                         wait(self.load_g(e))
 
@@ -450,14 +457,14 @@
     eng.stage([at("far"), at("far_o"), at("z1"), at("z1_o")], 2, False, False,
               [arrived(c_far, c_far_o), arrived(c_far_o), arrived(c_z1, c_z1_o + c_z1y + c_z2), arrived(c_z1_o)],
               ([keep_a], [Sent(c_got_a[0])]),
-              ((4, arrived(c_z1y + c_z2, c_z2y + c_z3 + c_z1y_o + c_z2_o)),),
+              ((5, arrived(c_z1y + c_z2, c_z2y + c_z3 + c_z1y_o + c_z2_o)),),
               [keep_b, c_got_b[0]], sum_a)
     sum_a.finish(n_loc - 1)
     sum_b = Adder(own_b, got_b, (chip_a, chip_b), held, add_in_sem, add_out_sem, arrived(c_got_b))
     eng.stage([at("z1y"), at("z1y_o"), at("z2"), at("z2_o")], 0, False, True,
               [nothing, arrived(c_z1y_o), nothing, arrived(c_z2_o)],
               ([keep_b], [Sent(c_got_b[0])]),
-              ((0, arrived(c_z2y + c_z3, c_z3y_y + c_z3y_z + c_z2y_o + c_z3_o)), (4, lambda: start(c_back)), (6, arrived(c_z3y_y, c_z3y_yo))), (), sum_b)
+              ((1, arrived(c_z2y + c_z3, c_z3y_y + c_z3y_z + c_z2y_o + c_z3_o)), (4, lambda: start(c_back)), (6, arrived(c_z3y_y, c_z3y_yo))), (), sum_b)
     sum_b.finish(n_loc - 1)
     arrived(c_z3y_z, c_z3y_zo)()
     arrived(c_z2y_o + c_z3_o + c_z3y_zo + c_z3y_yo + c_back)()
@@ -471,7 +478,7 @@
 
     def prelude():
         start(eng.load_w(0))
-        for e in (0, 1):
+        for e in range(4):
             start(eng.load_g(e))
 
     names = ("z2y", "z2y_o", "z3", "z3_o", "z3y", "z3y_o")

time: 284 us -> 289 us (1.018)
  Pallas kernels: 279 us -> 284 us
    pallas_call x2, Pallas kernels: 274 us -> 279 us  [call_kernel(): pl.pallas_call(functools.partial(kernel, cfg), in_specs=[pl.BlockSpec(mem...]
  transfers between devices with their start and end apart: 1 -> 1, of which waited for: 0 -> 0; matrix products, arithmetic and copies ran while one was open for 0% -> 0% of each run, Pallas kernels for 26% -> 27%
where the time goes in v3:
time: 289 us; the launch traced here: 288 us
  Pallas kernels  284 us (98%)
    pallas_call x2, Pallas kernels, call_kernel(): pl.pallas_call(functools.partial(kernel, cfg), in_specs=[pl.BlockSpec(mem...  279 us
  transfers between devices with their start and end apart: 1, of which 0 were waited for; matrix products, arithmetic and copies ran while one was open for 0% of the time, Pallas kernels for 27%

profile of v3, /device:TPU:0, one launch (start us, length us, event | category | flops | bytes accessed | tf_op | source)
XLA Modules:
  0.0 288.5 jit_solution(15823894264771367111)
XLA Ops:
  0.6 0.7 fusion.1
  1.4 0.7 reduce-precision_convert_fusion.1
  2.1 0.6 maximum_maximum_fusion.rg
  2.7 200.8 %roam.1 = (f32[8,1024,512]{2,1,0:T(8,128)}, f32[8,1024,512]{2,1,0:T(8,128)}, f32[8,512,1024]{2,1,0:T(8,128)}, bf16[15,1040,1024]{2,1,0:T(8,128)(2,1)}, f32[1024,...) custom-call(s32[1,1]{1,0:T(1,128)} %bitcast.lead_ref, ...), custom_call_target="tpu_custom_call" | custom-call | flops 6559891456 | bytes 104857600 | tf_op jit(solution)/shard_map/roam/pallas_call | solution.py:503
  203.5 1.6 collective-permute-start
  205.1 78.4 %rest.1 = (f32[8,1024,512]{2,1,0:T(8,128)}, f32[8,1024,512]{2,1,0:T(8,128)}, f32[8,512,1024]{2,1,0:T(8,128)}) custom-call(s32[1,1]{1,0:T(1,128)} %bitcast.lead_ref, bf16[15,1040,1024]{2,1,0:T(8,128)(2,1)} %get-tuple-element.22.land, bf16[8,1024,512]{2,1,0:T(8,128)(2,1)} %w1.3, bf16[8,1024,512]{2,1,0:T(8,128)(2,1)} %w3.3, bf16[8,512,1024]{2,1,0:T(8,128)(2,1)} %w2.3, ...), custom_call_target="tpu_custom_call" | custom-call | flops 6845104128 | bytes 104857600 | tf_op jit(solution)/shard_map/rest/pallas_call | solution.py:503
  283.5 0.0 collective-permute-done.b_ref
  283.5 4.8 %last.1 = (bf16[512,1024]{1,0:T(8,128)(2,1)}, bf16[512,1024]{1,0:T(8,128)(2,1)}) custom-call(f32[1024,1024]{1,0:T(8,128)} %get-tuple-element.17.m_ref, f32[256,1024]{1,0:T(8,128)} %get-tuple-element.18.a_ref, f32[768,1024]{1,0:T(8,128)} %collective-permute-done.b_ref), custom_call_target="tpu_custom_call" | custom-call | tf_op jit(solution)/shard_map/last/pallas_call | solution.py:539
Async XLA Ops:
  203.5 80.0 %collective-permute-start = (f32[768,1024]{1,0:T(8,128)}, f32[768,1024]{1,0:T(8,128)}, u32[]{:S(2)}, u32[]{:S(2)}) collective-permute-start(f32[768,1024]{1,0:T(8,128)} %get-tuple-element.19), channel_id=1, source_target_pairs={{0,2},{1,3},{2,0},{3,1},{4,6},{5,7},{6,4},{7,5},{8,10},{9,11},{10,... | collective-permute-start | bytes 9437192 | tf_op jit(solution)/shard_map/ppermute | solution.py:579

commit v4 on v3

--- a/solution.py
+++ b/solution.py
@@ -222,7 +222,7 @@
                         def _():
                             start(self.load_g(e + 2 - n_loc))
                     else:
-                        @pl.when(jnp.logical_and(e >= 2, e + 2 < n_loc))
+                        @pl.when(jnp.logical_and(e >= (2 if held else 0), e + 2 < n_loc))
                         def _():
                             start(self.load_g(e + 2))
 
@@ -478,7 +478,7 @@
 
     def prelude():
         start(eng.load_w(0))
-        for e in range(4):
+        for e in (0, 1):
             start(eng.load_g(e))
 
     names = ("z2y", "z2y_o", "z3", "z3_o", "z3y", "z3y_o")

time: 289 us -> 285 us (0.986)
  Pallas kernels: 284 us -> 280 us
    pallas_call x2, Pallas kernels: 279 us -> 275 us  [call_kernel(): pl.pallas_call(functools.partial(kernel, cfg), in_specs=[pl.BlockSpec(mem...]
  transfers between devices with their start and end apart: 1 -> 1, of which waited for: 0 -> 0; matrix products, arithmetic and copies ran while one was open for 0% -> 0% of each run, Pallas kernels for 27% -> 26%
where the time goes in v4:
time: 285 us
  Pallas kernels  280 us (98%)
    pallas_call x2, Pallas kernels, call_kernel(): pl.pallas_call(functools.partial(kernel, cfg), in_specs=[pl.BlockSpec(mem...  275 us
  transfers between devices with their start and end apart: 1, of which 0 were waited for; matrix products, arithmetic and copies ran while one was open for 0% of the time, Pallas kernels for 26%

profile of v4, /device:TPU:0, one launch (start us, length us, event | category | flops | bytes accessed | tf_op | source)
XLA Modules:
  0.0 284.7 jit_solution(5534181595026512943)
XLA Ops:
  0.6 0.7 fusion.1
  1.4 0.7 reduce-precision_convert_fusion.1
  2.1 0.6 maximum_maximum_fusion.rg
  2.7 200.8 %roam.1 = (f32[8,1024,512]{2,1,0:T(8,128)}, f32[8,1024,512]{2,1,0:T(8,128)}, f32[8,512,1024]{2,1,0:T(8,128)}, bf16[15,1040,1024]{2,1,0:T(8,128)(2,1)}, f32[1024,...) custom-call(s32[1,1]{1,0:T(1,128)} %bitcast.lead_ref, ...), custom_call_target="tpu_custom_call" | custom-call | flops 6559891456 | bytes 104857600 | tf_op jit(solution)/shard_map/roam/pallas_call | solution.py:503
  203.5 1.6 collective-permute-start
  205.1 74.6 %rest.1 = (f32[8,1024,512]{2,1,0:T(8,128)}, f32[8,1024,512]{2,1,0:T(8,128)}, f32[8,512,1024]{2,1,0:T(8,128)}) custom-call(s32[1,1]{1,0:T(1,128)} %bitcast.lead_ref, bf16[15,1040,1024]{2,1,0:T(8,128)(2,1)} %get-tuple-element.22.land, bf16[8,1024,512]{2,1,0:T(8,128)(2,1)} %w1.3, bf16[8,1024,512]{2,1,0:T(8,128)(2,1)} %w3.3, bf16[8,512,1024]{2,1,0:T(8,128)(2,1)} %w2.3, ...), custom_call_target="tpu_custom_call" | custom-call | flops 6845104128 | bytes 104857600 | tf_op jit(solution)/shard_map/rest/pallas_call | solution.py:503
  279.7 0.0 collective-permute-done.b_ref
  279.7 4.8 %last.1 = (bf16[512,1024]{1,0:T(8,128)(2,1)}, bf16[512,1024]{1,0:T(8,128)(2,1)}) custom-call(f32[1024,1024]{1,0:T(8,128)} %get-tuple-element.17.m_ref, f32[256,1024]{1,0:T(8,128)} %get-tuple-element.18.a_ref, f32[768,1024]{1,0:T(8,128)} %collective-permute-done.b_ref), custom_call_target="tpu_custom_call" | custom-call | tf_op jit(solution)/shard_map/last/pallas_call | solution.py:539
Async XLA Ops:
  203.5 76.2 %collective-permute-start = (f32[768,1024]{1,0:T(8,128)}, f32[768,1024]{1,0:T(8,128)}, u32[]{:S(2)}, u32[]{:S(2)}) collective-permute-start(f32[768,1024]{1,0:T(8,128)} %get-tuple-element.19), channel_id=1, source_target_pairs={{0,2},{1,3},{2,0},{3,1},{4,6},{5,7},{6,4},{7,5},{8,10},{9,11},{10,... | collective-permute-start | bytes 9437192 | tf_op jit(solution)/shard_map/ppermute | solution.py:579

commit v5 on v4

--- a/solution.py
+++ b/solution.py
@@ -384,7 +384,7 @@
         self.saved(last)
 
 
-def roam_kernel(cfg, lead_ref, tokens, grad_y, rg, w1, w3, w2, g1, g3, g2, land, own_a, own_b, got_a, got_b, mine, chip_a, chip_b, back_a, *scratch):
+def roam_kernel(cfg, lead_ref, tokens, grad_y, rg, w1, w3, w2, g1, g3, g2, land, own_a, own_b, got_a, got_b, chip_a, chip_b, back_a, *scratch):
     send_sem, recv_sem, part_sem, held, add_in_sem, add_out_sem = scratch[-6:]
     eng = Engine(cfg, lead_ref[0, 0], (w1, w3, w2), (g1, g3, g2), (g1, g3, g2), scratch[:-6], 2)
     q, r = lax.axis_index("data"), lax.axis_index("expert")
@@ -414,8 +414,9 @@
     def onward(src, dst, device):
         return [remote(at(src), at(dst), device)]
 
-    cut = (2 * tok + RG_ROWS) // 64 * 48
-    upper, lower = pl.ds(0, cut), pl.ds(cut, 2 * tok + RG_ROWS - cut)
+    cut = (2 * tok + RG_ROWS) // 16 // 16 * 11 * 16
+    upper = [pl.ds(0, tok), pl.ds(tok, cut - tok)]
+    lower = pl.ds(cut, 2 * tok + RG_ROWS - cut)
     c_back = [remote(chip_a, back_a, across)]
     c_other, c_far, c_z1 = first("other", partner), first("far", across), first("z1", znext)
     c_far_o, c_z1_o = onward("far", "far_o", partner), onward("z1", "z1_o", partner)
@@ -423,9 +424,9 @@
     c_z1y_o, c_z2_o = onward("z1y", "z1y_o", partner), onward("z2", "z2_o", partner)
     c_z2y, c_z3 = onward("z2", "z2y", across), onward("z2", "z3", znext)
     c_z2y_o, c_z3_o = onward("z2y", "z2y_o", partner), onward("z3", "z3_o", partner)
-    c_z3y_z = [remote(at("far", upper), at("z3y", upper), zprev)]
+    c_z3y_z = [remote(at("far", rows), at("z3y", rows), zprev) for rows in upper]
     c_z3y_y = [remote(at("z3", lower), at("z3y", lower), across)]
-    c_z3y_zo = [remote(at("z3y", upper), at("z3y_o", upper), partner)]
+    c_z3y_zo = [remote(at("z3y", rows), at("z3y_o", rows), partner) for rows in upper]
     c_z3y_yo = [remote(at("z3y", lower), at("z3y_o", lower), partner)]
     c_got_a, c_got_b = [remote(eng.g13.at[3], got_a, partner)], [remote(eng.g13.at[3], got_b, partner)]
     keep_a = pltpu.make_async_copy(eng.g13.at[2], own_a, part_sem.at[0])
@@ -453,21 +454,19 @@
     start(c_other + c_far + c_z1)
     eng.stage([(tokens, grad_y, rg), at("other")], 2, True, False, [nothing, arrived(c_other)], (), (), [keep_a, c_got_a[0]],
               prelude=lambda: start(eng.load_w(0)))
-    sum_a = Adder(own_a, got_a, (None, mine), held, add_in_sem, add_out_sem, arrived(c_got_a))
     eng.stage([at("far"), at("far_o"), at("z1"), at("z1_o")], 2, False, False,
               [arrived(c_far, c_far_o), arrived(c_far_o), arrived(c_z1, c_z1_o + c_z1y + c_z2), arrived(c_z1_o)],
               ([keep_a], [Sent(c_got_a[0])]),
               ((5, arrived(c_z1y + c_z2, c_z2y + c_z3 + c_z1y_o + c_z2_o)),),
-              [keep_b, c_got_b[0]], sum_a)
-    sum_a.finish(n_loc - 1)
+              [keep_b, c_got_b[0]])
     sum_b = Adder(own_b, got_b, (chip_a, chip_b), held, add_in_sem, add_out_sem, arrived(c_got_b))
     eng.stage([at("z1y"), at("z1y_o"), at("z2"), at("z2_o")], 0, False, True,
               [nothing, arrived(c_z1y_o), nothing, arrived(c_z2_o)],
               ([keep_b], [Sent(c_got_b[0])]),
-              ((1, arrived(c_z2y + c_z3, c_z3y_y + c_z3y_z + c_z2y_o + c_z3_o)), (4, lambda: start(c_back)), (6, arrived(c_z3y_y, c_z3y_yo))), (), sum_b)
+              ((1, arrived(c_z2y + c_z3, c_z3y_y + c_z3y_z + c_z2y_o + c_z3_o)), (4, lambda: start(c_back)), (6, arrived(c_z3y_y + c_z3y_z[:1], c_z3y_yo + c_z3y_zo[:1]))), (), sum_b)
+    arrived(c_z3y_z[1:], c_z3y_zo[1:])()
     sum_b.finish(n_loc - 1)
-    arrived(c_z3y_z, c_z3y_zo)()
-    arrived(c_z2y_o + c_z3_o + c_z3y_zo + c_z3y_yo + c_back)()
+    arrived(c_z2y_o + c_z3_o + c_z3y_zo + c_z3y_yo + c_back + c_got_a)()
     for c in flights:
         if c is not c_got_a[0] and c is not c_got_b[0]:
             c.wait_send()
@@ -512,11 +511,11 @@
     )(*args)
 
 
-def last_sum(mine, back_a, back_b, tok, d_model):
+def last_sum(own_a, got_a, back_a, back_b, tok, d_model):
     rows = back_a.shape[0] // 2
     n_all, n_half = 2 * tok // rows, tok // rows
 
-    def kernel(m_ref, a_ref, b_ref, y_ref, x_ref, m, v, out, in_sem, out_sem):
+    def kernel(m_ref, n_ref, a_ref, b_ref, y_ref, x_ref, m, n, v, out, in_sem, out_sem):
         def piece(ref, j):
             return ref.at[pl.ds(j * rows, rows)]
 
@@ -524,27 +523,28 @@
         for j in range(n_all):
             other = piece(a_ref, j) if j < 2 else piece(b_ref, j - 2)
             loads.append([pltpu.make_async_copy(piece(m_ref, j), m.at[j], in_sem.at[j, 0]),
-                          pltpu.make_async_copy(other, v.at[j], in_sem.at[j, 1])])
+                          pltpu.make_async_copy(piece(n_ref, j), n.at[j], in_sem.at[j, 1]),
+                          pltpu.make_async_copy(other, v.at[j], in_sem.at[j, 2])])
             place = piece(y_ref, j) if j < n_half else piece(x_ref, j - n_half)
             saves.append(pltpu.make_async_copy(out.at[j], place, out_sem.at[j]))
         for copies in loads:
             start(copies)
         for j in range(n_all):
             wait(loads[j])
-            out[j] = (m[j] + v[j]).astype(BF16)
+            out[j] = (m[j] + n[j] + v[j]).astype(BF16)
             saves[j].start()
         wait(saves)
 
     dma = pltpu.SemaphoreType.DMA
     return pl.pallas_call(
         kernel,
-        in_specs=[pl.BlockSpec(memory_space=pl.ANY)] * 3,
+        in_specs=[pl.BlockSpec(memory_space=pl.ANY)] * 4,
         out_specs=[pl.BlockSpec(memory_space=pl.ANY)] * 2,
         out_shape=[jax.ShapeDtypeStruct((tok, d_model), BF16)] * 2,
-        scratch_shapes=[pltpu.VMEM((n_all, rows, d_model), F32)] * 2 + [pltpu.VMEM((n_all, rows, d_model), BF16), dma((n_all, 2)), dma((n_all,))],
+        scratch_shapes=[pltpu.VMEM((n_all, rows, d_model), F32)] * 3 + [pltpu.VMEM((n_all, rows, d_model), BF16), dma((n_all, 3)), dma((n_all,))],
         compiler_params=pltpu.CompilerParams(vmem_limit_bytes=67_000_000),
         name="last",
-    )(mine, back_a, back_b)
+    )(own_a, got_a, back_a, back_b)
 
 
 def solution(mesh):
@@ -568,17 +568,17 @@
         rg = jnp.concatenate([jnp.concatenate([routes.T.astype(F32), hi], 0), jnp.concatenate([mid, low], 0)], 1).astype(BF16)
         weights = (w_in1, w_in3, w_out)
         grads = [jax.ShapeDtypeStruct(w.shape, F32) for w in weights]
-        sums = [jax.ShapeDtypeStruct((2 * tok, d_model), F32)] * 6
+        sums = [jax.ShapeDtypeStruct((2 * tok, d_model), F32)] * 4
         land = jax.ShapeDtypeStruct((len(BLOCKS), 2 * tok + RG_ROWS, d_model), BF16)
         dma, n_fly, quarter = pltpu.SemaphoreType.DMA, 28, 2 * (2 * tok // n_loc)
-        sums[5:] = [jax.ShapeDtypeStruct((n, d_model), F32) for n in (quarter, 2 * tok - quarter, quarter)]
-        *acc, land, _, _, _, _, mine, _, chip_b, back_a = call_kernel(
+        sums += [jax.ShapeDtypeStruct((n, d_model), F32) for n in (quarter, 2 * tok - quarter, quarter)]
+        *acc, land, own_a, _, got_a, _, _, chip_b, back_a = call_kernel(
             "roam", roam_kernel, cfg, [lead, tokens, grad_y, rg, *weights], [*grads, land, *sums], 4, 2,
             [dma((n_fly,)), dma((n_fly,)), dma((2,)), pltpu.VMEM((2, 2, 2 * tok // n_loc, d_model), F32), dma((2, 2)), dma((2,))],
             dict(collective_id=0, has_side_effects=True))
         back_b = lax.ppermute(chip_b, "expert", across)
         acc1, acc3, acc2 = call_kernel("rest", rest_kernel, cfg, [lead, land, *weights, *acc], grads, 6, 0, [], {})
-        y_out, grad_x = last_sum(mine, back_a, back_b, tok, d_model)
+        y_out, grad_x = last_sum(own_a, got_a, back_a, back_b, tok, d_model)
         return y_out, grad_x, acc1, acc3, acc2
 
     return jax.shard_map(body, mesh=mesh,

time: 285 us -> 286 us (level)
  no operation moved by 1% of the time
where the time goes in v5:
time: 286 us
  Pallas kernels  281 us (98%)
    pallas_call x2, Pallas kernels, call_kernel(): pl.pallas_call(functools.partial(kernel, cfg), in_specs=[pl.BlockSpec(mem...  275 us
    pallas_call x1, Pallas kernels, last_sum(): pl.pallas_call(kernel, in_specs=[pl.BlockSpec(memory_space=pl.ANY)] * 4,...  6.19 us
  transfers between devices with their start and end apart: 1, of which 0 were waited for; matrix products, arithmetic and copies ran while one was open for 0% of the time, Pallas kernels for 26%

profile of v5, /device:TPU:0, one launch (start us, length us, event | category | flops | bytes accessed | tf_op | source)
XLA Modules:
  0.0 285.8 jit_solution(16510217956916576964)
XLA Ops:
  0.6 0.7 fusion.1
  1.4 0.7 reduce-precision_convert_fusion.1
  2.1 0.6 maximum_maximum_fusion.rg
  2.7 200.5 %roam.1 = (f32[8,1024,512]{2,1,0:T(8,128)}, f32[8,1024,512]{2,1,0:T(8,128)}, f32[8,512,1024]{2,1,0:T(8,128)}, bf16[15,1040,1024]{2,1,0:T(8,128)(2,1)}, f32[1024,...) custom-call(s32[1,1]{1,0:T(1,128)} %bitcast.lead_ref, ...), custom_call_target="tpu_custom_call" | custom-call | flops 6559891456 | bytes 104857600 | tf_op jit(solution)/shard_map/roam/pallas_call | solution.py:502
  203.2 1.6 collective-permute-start
  204.8 74.6 %rest.1 = (f32[8,1024,512]{2,1,0:T(8,128)}, f32[8,1024,512]{2,1,0:T(8,128)}, f32[8,512,1024]{2,1,0:T(8,128)}) custom-call(s32[1,1]{1,0:T(1,128)} %bitcast.lead_ref, bf16[15,1040,1024]{2,1,0:T(8,128)(2,1)} %get-tuple-element.24.land, bf16[8,1024,512]{2,1,0:T(8,128)(2,1)} %w1.3, bf16[8,1024,512]{2,1,0:T(8,128)(2,1)} %w3.3, bf16[8,512,1024]{2,1,0:T(8,128)(2,1)} %w2.3, ...), custom_call_target="tpu_custom_call" | custom-call | flops 6845104128 | bytes 104857600 | tf_op jit(solution)/shard_map/rest/pallas_call | solution.py:502
  279.4 0.0 collective-permute-done.b_ref
  279.4 6.2 %last.1 = (bf16[512,1024]{1,0:T(8,128)(2,1)}, bf16[512,1024]{1,0:T(8,128)(2,1)}) custom-call(f32[1024,1024]{1,0:T(8,128)} %get-tuple-element.18.m_ref, f32[1024,1024]{1,0:T(8,128)} %get-tuple-element.19.n_ref, f32[256,1024]{1,0:T(8,128)} %get-tuple-element.20.a_ref, f32[768,1024]{1,0:T(8,128)} %collective-permute-done.b_ref), custom_call_target="tpu_custom_call" | custom-call | tf_op jit(solution)/shard_map/last/pallas_call | solution.py:539
Async XLA Ops:
  203.2 76.2 %collective-permute-start = (f32[768,1024]{1,0:T(8,128)}, f32[768,1024]{1,0:T(8,128)}, u32[]{:S(2)}, u32[]{:S(2)}) collective-permute-start(f32[768,1024]{1,0:T(8,128)} %get-tuple-element.21), channel_id=1, source_target_pairs={{0,2},{1,3},{2,0},{3,1},{4,6},{5,7},{6,4},{7,5},{8,10},{9,11},{10,... | collective-permute-start | bytes 9437192 | tf_op jit(solution)/shard_map/ppermute | solution.py:579

commit v6 on v2

--- a/solution.py
+++ b/solution.py
@@ -125,7 +125,7 @@
         dab[0:rows, 0:d_ff] = (dh * b * sig * (1.0 + a * (1.0 - sig))).astype(BF16)
         dab[0:rows, d_ff:] = (dh * act).astype(BF16)
         middle()
-        if size < self.cap:
+        if size < self.cap and n_src <= 4:
             def columns(k, carry):
                 cols = pl.ds(pl.multiple_of(k * d_ff, d_ff), d_ff)
                 self.g13[g, :, cols] = self.g13[g, :, cols] + dot_tn(load(self.rows_x), dab[0:rows, cols])
@@ -407,8 +407,9 @@
     def onward(src, dst, device):
         return [remote(at(src), at(dst), device)]
 
-    cut = (2 * tok + RG_ROWS) // 64 * 48
-    upper, lower = pl.ds(0, cut), pl.ds(cut, 2 * tok + RG_ROWS - cut)
+    cut = (2 * tok + RG_ROWS) // 16 // 16 * 11 * 16
+    upper = [pl.ds(0, tok), pl.ds(tok, cut - tok)]
+    lower = pl.ds(cut, 2 * tok + RG_ROWS - cut)
     c_back = [remote(chip_a, back_a, across)]
     c_other, c_far, c_z1 = first("other", partner), first("far", across), first("z1", znext)
     c_far_o, c_z1_o = onward("far", "far_o", partner), onward("z1", "z1_o", partner)
@@ -416,9 +417,9 @@
     c_z1y_o, c_z2_o = onward("z1y", "z1y_o", partner), onward("z2", "z2_o", partner)
     c_z2y, c_z3 = onward("z2", "z2y", across), onward("z2", "z3", znext)
     c_z2y_o, c_z3_o = onward("z2y", "z2y_o", partner), onward("z3", "z3_o", partner)
-    c_z3y_z = [remote(at("far", upper), at("z3y", upper), zprev)]
+    c_z3y_z = [remote(at("far", rows), at("z3y", rows), zprev) for rows in upper]
     c_z3y_y = [remote(at("z3", lower), at("z3y", lower), across)]
-    c_z3y_zo = [remote(at("z3y", upper), at("z3y_o", upper), partner)]
+    c_z3y_zo = [remote(at("z3y", rows), at("z3y_o", rows), partner) for rows in upper]
     c_z3y_yo = [remote(at("z3y", lower), at("z3y_o", lower), partner)]
     c_got_a, c_got_b = [remote(eng.g13.at[3], got_a, partner)], [remote(eng.g13.at[3], got_b, partner)]
     keep_a = pltpu.make_async_copy(eng.g13.at[2], own_a, part_sem.at[0])
@@ -457,9 +458,9 @@
     eng.stage([at("z1y"), at("z1y_o"), at("z2"), at("z2_o")], 0, False, True,
               [nothing, arrived(c_z1y_o), nothing, arrived(c_z2_o)],
               ([keep_b], [Sent(c_got_b[0])]),
-              ((0, arrived(c_z2y + c_z3, c_z3y_y + c_z3y_z + c_z2y_o + c_z3_o)), (4, lambda: start(c_back)), (6, arrived(c_z3y_y, c_z3y_yo))), (), sum_b)
+              ((0, arrived(c_z2y + c_z3, c_z3y_y + c_z3y_z + c_z2y_o + c_z3_o)), (4, lambda: start(c_back)), (6, arrived(c_z3y_y + c_z3y_z[:1], c_z3y_yo + c_z3y_zo[:1]))), (), sum_b)
     sum_b.finish(n_loc - 1)
-    arrived(c_z3y_z, c_z3y_zo)()
+    arrived(c_z3y_z[1:], c_z3y_zo[1:])()
     arrived(c_z2y_o + c_z3_o + c_z3y_zo + c_z3y_yo + c_back)()
     for c in flights:
         if c is not c_got_a[0] and c is not c_got_b[0]:

time: 284 us -> 284 us (level)
  no operation moved by 1% of the time
where the time goes in v6:
time: 284 us
  Pallas kernels  279 us (98%)
    pallas_call x2, Pallas kernels, call_kernel(): pl.pallas_call(functools.partial(kernel, cfg), in_specs=[pl.BlockSpec(mem...  274 us
  transfers between devices with their start and end apart: 1, of which 0 were waited for; matrix products, arithmetic and copies ran while one was open for 0% of the time, Pallas kernels for 26%

profile of v6, /device:TPU:0, one launch (start us, length us, event | category | flops | bytes accessed | tf_op | source)
XLA Modules:
  0.0 283.5 jit_solution(15327692501695106984)
XLA Ops:
  0.6 0.7 fusion.1
  1.4 0.7 reduce-precision_convert_fusion.1
  2.1 0.6 maximum_maximum_fusion.rg
  2.7 199.8 %roam.1 = (f32[8,1024,512]{2,1,0:T(8,128)}, f32[8,1024,512]{2,1,0:T(8,128)}, f32[8,512,1024]{2,1,0:T(8,128)}, bf16[15,1040,1024]{2,1,0:T(8,128)(2,1)}, f32[1024,...) custom-call(s32[1,1]{1,0:T(1,128)} %bitcast.lead_ref, ...), custom_call_target="tpu_custom_call" | custom-call | flops 6559891456 | bytes 104857600 | tf_op jit(solution)/shard_map/roam/pallas_call | solution.py:497
  202.5 1.6 collective-permute-start
  204.1 74.4 %rest.1 = (f32[8,1024,512]{2,1,0:T(8,128)}, f32[8,1024,512]{2,1,0:T(8,128)}, f32[8,512,1024]{2,1,0:T(8,128)}) custom-call(s32[1,1]{1,0:T(1,128)} %bitcast.lead_ref, bf16[15,1040,1024]{2,1,0:T(8,128)(2,1)} %get-tuple-element.22.land, bf16[8,1024,512]{2,1,0:T(8,128)(2,1)} %w1.3, bf16[8,1024,512]{2,1,0:T(8,128)(2,1)} %w3.3, bf16[8,512,1024]{2,1,0:T(8,128)(2,1)} %w2.3, ...), custom_call_target="tpu_custom_call" | custom-call | flops 6845104128 | bytes 104857600 | tf_op jit(solution)/shard_map/rest/pallas_call | solution.py:497
  278.5 0.0 collective-permute-done.b_ref
  278.5 4.8 %last.1 = (bf16[512,1024]{1,0:T(8,128)(2,1)}, bf16[512,1024]{1,0:T(8,128)(2,1)}) custom-call(f32[1024,1024]{1,0:T(8,128)} %get-tuple-element.17.m_ref, f32[256,1024]{1,0:T(8,128)} %get-tuple-element.18.a_ref, f32[768,1024]{1,0:T(8,128)} %collective-permute-done.b_ref), custom_call_target="tpu_custom_call" | custom-call | tf_op jit(solution)/shard_map/last/pallas_call | solution.py:533
Async XLA Ops:
  202.5 76.0 %collective-permute-start = (f32[768,1024]{1,0:T(8,128)}, f32[768,1024]{1,0:T(8,128)}, u32[]{:S(2)}, u32[]{:S(2)}) collective-permute-start(f32[768,1024]{1,0:T(8,128)} %get-tuple-element.19), channel_id=1, source_target_pairs={{0,2},{1,3},{2,0},{3,1},{4,6},{5,7},{6,4},{7,5},{8,10},{9,11},{10,... | collective-permute-start | bytes 9437192 | tf_op jit(solution)/shard_map/ppermute | solution.py:573
